TPU v7x, 32 devices: a whole 2x2x4 slice. The times are simulated.
32 devices in a mesh: parts: 2 (over y), mem: 4 (over z), space: 4 (over x, core).
Axes of the slice: x: 2, y: 2, z: 4, core: 2. Of those that a mesh axis runs over, the one named last changes fastest.
Arguments:
- ensemble: bfloat16 [64, 70, 8192], P('mem', None, ('parts', 'space')), parts along dimension 2, may hold values from -6 to 6
- transform: bfloat16 [128, 64], P('parts'), parts along dimension 0, may hold values from -0.75 to 0.75
- obs_operator: bfloat16 [16, 70], replicated, may hold values from -0.75 to 0.75
- obs_weight: float32 [16, 8192], P(None, ('parts', 'space')), parts along dimension 1, may hold values from 0.25 to 40, as said below
Outputs:
- analysis: bfloat16 [64, 70, 8192], P('mem', None, ('parts', 'space')), parts along dimension 2
- prior_gram: float32 [128, 64], P('parts'), parts along dimension 0
- posterior_gram: float32 [128, 64], P('parts'), parts along dimension 0
There are 2 independent parts, one for each index of `parts`. A program takes and returns all parts, laid end to end along the dimension named above; an argument that names none is the same for every part. Nothing has to cross between parts.
Inputs may be any that keep to these rules, and one draw needn't show every extreme that they name: `obs_weight`: positive.
All inputs are finite; a program needn't handle non-finite values.
Results may differ from a plain program's by a relative error of at most 0.001.
Values may be sent and summed in bfloat16 or wider, within the bound.
A program may use at most 64 MiB of HBM per device.

v0:
```python
import jax
import jax.numpy as jnp
from jax import lax
from jax.sharding import PartitionSpec as P

MEMBERS = 64
HIGHEST = lax.Precision.HIGHEST


def gram_terms(observed, weights):
    departures = observed - jnp.sum(observed, axis=0) / MEMBERS
    weighted = departures * weights[None, :, :]
    partial_gram = jnp.einsum("ioc,joc->ij", weighted, departures, precision=HIGHEST)
    return (partial_gram, jnp.sum(weights))


def per_device(ensemble, transform, obs_operator, obs_weight):
    local_members = ensemble.shape[0]
    mixing = transform.astype(jnp.float32)
    own_start = lax.axis_index("mem") * local_members
    own_columns = lax.dynamic_slice_in_dim(transform, own_start, local_members, 1)
    keep_mean = 1.0 - jnp.sum(own_columns.astype(jnp.float32), axis=0)
    members_block = lax.all_gather(ensemble, "mem", axis=0, tiled=True)
    combined = jnp.einsum(
        "kj,kvc->jvc", own_columns, members_block, preferred_element_type=jnp.float32
    )
    totals = jnp.sum(members_block, axis=0, dtype=jnp.float32)
    results = (totals, combined)
    totals = results[0]
    combined = results[1]
    member_mean = totals / MEMBERS
    analysis = (combined + member_mean[None, :, :] * keep_mean[:, None, None]).astype(jnp.bfloat16)
    observed = jnp.einsum("ov,mvc->moc", obs_operator, ensemble, preferred_element_type=jnp.float32)
    by_columns = lax.all_to_all(
        observed.astype(jnp.bfloat16), "mem", split_axis=2, concat_axis=0, tiled=True
    ).astype(observed.dtype)
    cells_here = by_columns.shape[2]
    own_weights = lax.dynamic_slice_in_dim(
        obs_weight, lax.axis_index("mem") * cells_here, cells_here, 1
    )
    partial_gram, weight_sum = gram_terms(by_columns, own_weights)
    gram_sum, weight_total = lax.psum((partial_gram, weight_sum), ("mem", "space"))
    prior_gram = gram_sum / weight_total
    carried = jnp.dot(mixing.T, prior_gram, precision=HIGHEST)
    posterior_gram = jnp.dot(carried, mixing, precision=HIGHEST)
    return (analysis, prior_gram, posterior_gram)


def solution(mesh):
    return jax.shard_map(
        per_device,
        mesh=mesh,
        in_specs=(
            P("mem", None, ("parts", "space")),
            P("parts", None),
            P(),
            P(None, ("parts", "space")),
        ),
        out_specs=(P("mem", None, ("parts", "space")), P("parts", None), P("parts", None)),
        check_vma=False,
    )
```

profile of v0, /device:TPU:0, one launch (start us, length us, event | category | flops | bytes accessed | tf_op | source)
XLA Modules:
  0.0 202.9 jit_solution(353153275937876548)
XLA Ops:
  7.2 0.0 copy-start
  7.2 0.0 all-gather.2.cloned.1.call-start
  7.2 0.7 all-gather.2.cloned.1.call-update
  7.9 3.0 %fusion.7 = bf16[16,16,1024]{2,1,0:T(8,128)(2,1)S(1)} fusion(bf16[16,70,1024]{2,0,1:T(8,128)(2,1)} %param.4, bf16[16,70]{1,0:T(8,128)(2,1)} %param.6), kind=kOutput, calls=%fused_computation.8 | convolution fusion | flops 36962304 | bytes 2820288 | tf_op jit(solution)/shard_map/ov,mvc->moc/dot_general | solution.py:33
  10.9 4.7 %copy.25 = bf16[16,16,1024]{1,0,2:T(8,128)(2,1)} copy(bf16[16,16,1024]{2,1,0:T(8,128)(2,1)S(1)} %fusion.7) | data formatting | bytes 1048576 | tf_op jit(solution)/shard_map/convert_element_type | solution.py:35
  15.6 6.6 %reshape.27 = bf16[4,2,32768]{2,1,0:T(2,128)(2,1)} reshape(bf16[1024,16,16]{2,1,0:T(8,128)(2,1)} %bitcast.28) | data formatting | bytes 1048576
  22.2 6.4 %all-to-all-start = ((bf16[4,2,32768]{2,1,0:T(2,128)(2,1)}), bf16[4,2,32768]{2,1,0:T(2,128)(2,1)S(1)}, u32[]{:S(2)}, u32[]{:S(2)}) async-start(bf16[4,2,32768]{2,1,0:T(2,128)(2,1)} %reshape.27), calls=%async_computation | async-start | bytes 1048576 | tf_op jit(solution)/shard_map/all_to_all | solution.py:34
  28.6 0.0 copy-done
  28.6 0.1 constant_dynamic-slice_fusion.1
  28.7 0.1 copy.28
  28.8 0.1 convert_reduce_fusion.2
  28.9 1.3 fusion.16
  30.2 25.9 %all-to-all-done = bf16[4,2,32768]{2,1,0:T(2,128)(2,1)S(1)} async-done(((bf16[4,2,32768]{2,1,0:T(2,128)(2,1)}), bf16[4,2,32768]{2,1,0:T(2,128)(2,1)S(1)}, u32[]{:S(2)}, u32[]{:S(2)}) %all-to-all-start) | async-done | bytes 524320 | tf_op jit(solution)/shard_map/all_to_all | solution.py:34
  56.1 4.1 %reshape.28 = bf16[1024,16,16]{2,1,0:T(8,128)(2,1)} reshape(bf16[4,2,32768]{2,1,0:T(2,128)(2,1)S(1)} %all-to-all-done) | data formatting | bytes 1048576
  60.2 6.1 %bitcast_convert_fusion = f32[16,16,1024]{1,0,2:T(8,128)} fusion(bf16[1024,16,16]{2,1,0:T(8,128)(2,1)} %reshape.28), kind=kLoop, calls=%fused_computation.22 | loop fusion | flops 262144 | bytes 1572864 | tf_op jit(solution)/shard_map/convert_element_type | solution.py:36
  66.4 6.6 %copy.26 = f32[4,16,16,256]{3,1,0,2:T(8,128)S(1)} copy(f32[4,16,16,256]{2,1,3,0:T(8,128)} %bitcast.27) | data formatting | bytes 2097152 | tf_op jit(solution)/shard_map/convert_element_type | solution.py:36
  72.9 4.2 %convert_reduce_fusion.1 = f32[16,1024]{0,1:T(8,128)S(1)} fusion(bf16[1024,16,16]{2,1,0:T(8,128)(2,1)} %reshape.28), kind=kLoop, calls=%fused_computation.4 | loop fusion | flops 507904 | bytes 589824 | tf_op jit(solution)/shard_map/reduce_sum | solution.py:11
  77.2 0.1 copy.27
  77.3 0.1 bitcast_subtract_fusion
  77.5 1.0 fusion.10
  78.5 63.8 %all-reduce = (f32[64,64]{1,0:T(8,128)S(1)}, f32[]{:T(128)}) all-reduce(f32[64,64]{1,0:T(8,128)S(1)} %fusion.10, f32[]{:T(128)} %get-tuple-element.5), channel_id=1, replica_groups=mesh['parts'=2,'mem'=4,'space'=4] {'mem','space'}, use_global_device_ids=true, to_apply=%region_4.0 | all-reduce | flops 4097 | bytes 32776 | tf_op jit(solution)/shard_map/psum | solution.py:42
  142.3 0.7 broadcast_divide_fusion
  142.9 0.0 copy-start.2
  142.9 0.2 fusion.17
  143.2 0.8 fusion.18
  144.0 42.6 %all-gather.2.cloned.1.call-done = bf16[64,70,1024]{2,0,1:T(8,128)(2,1)} async-done(((bf16[16,70,1024]{2,0,1:T(8,128)(2,1)}), bf16[64,70,1024]{2,0,1:T(8,128)(2,1)}) %all-gather.2.cloned.1.call-update) | async-done | bytes 9175056 | tf_op jit(solution)/shard_map/all_gather | solution.py:23
  186.6 0.0 copy-start.1
  186.6 6.7 %convert_reduce_fusion = f32[70,1024]{1,0:T(8,128)S(1)} fusion(bf16[64,70,1024]{2,0,1:T(8,128)(2,1)} %all-gather.2.cloned.1.call-done), kind=kLoop, calls=%fused_computation | loop fusion | flops 9103360 | bytes 9461760 | tf_op jit(solution)/shard_map/reduce_sum | solution.py:27
  193.3 0.0 copy-done.2
  193.3 0.0 copy-done.1
  193.3 2.8 %add_convert_fusion = bf16[16,70,1024]{2,0,1:T(8,128)(2,1)} fusion(f32[16]{0:T(128)S(1)} %broadcast_subtract_fusion, f32[70,1024]{1,0:T(8,128)S(1)} %broadcast_multiply_fusion, bf16[64,70,1024]{2,0,1:T(8,128)(2,1)S(1)} %copy-done.1, bf16[64,16]{1,0:T(8,128)(2,1)S(1)} %constant_dynamic-slice_fusion.1), kind=kOutput, calls=%fused_computation.1 | convolution fusion | flops 150241280 | bytes 11757632 | tf_op jit(solution)/shard_map/kj,kvc->jvc/dot_general | solution.py:24
  (4 shorter events, 0.1 us)
Async XLA Ops:
  7.2 21.4 %copy-start = (bf16[64,64]{1,0:T(8,128)(2,1)S(1)}, bf16[64,64]{1,0:T(8,128)(2,1)}, u32[]{:S(2)}) copy-start(bf16[64,64]{1,0:T(8,128)(2,1)} %param.5) | copy-start | bytes 24580
  7.2 179.4 %all-gather.2.cloned.1.call-start = ((), (), s32[]{:S(2)}) async-start(), calls=%async_computation.1 | async-start | bytes 11468800 | tf_op jit(solution)/shard_map/all_gather | solution.py:23
  22.2 33.9 %all-to-all-start = ((bf16[4,2,32768]{2,1,0:T(2,128)(2,1)}), bf16[4,2,32768]{2,1,0:T(2,128)(2,1)S(1)}, u32[]{:S(2)}, u32[]{:S(2)}) async-start(bf16[4,2,32768]{2,1,0:T(2,128)(2,1)} %reshape.27), calls=%async_computation | async-start | bytes 1048576 | tf_op jit(solution)/shard_map/all_to_all | solution.py:34
  142.9 50.3 %copy-start.2 = (f32[64,64]{1,0:T(8,128)}, f32[64,64]{1,0:T(8,128)S(1)}, u32[]{:S(2)}) copy-start(f32[64,64]{1,0:T(8,128)S(1)} %broadcast_divide_fusion) | copy-start | bytes 49156
  186.6 6.7 %copy-start.1 = (bf16[64,70,1024]{2,0,1:T(8,128)(2,1)S(1)}, bf16[64,70,1024]{2,0,1:T(8,128)(2,1)}, u32[]{:S(2)}) copy-start(bf16[64,70,1024]{2,0,1:T(8,128)(2,1)} %all-gather.2.cloned.1.call-done) | copy-start | bytes 27525124
Sparse Core Ops, SparseCore 0:
  9.6 176.9 all-gather.1
where the time goes:
time: 203 us
  waiting for transfers between devices  69.2 us (34%)
  blocking collectives  63.8 us (31%)
  local copies, waits for them, and re-layouts  22.2 us (11%)
  other arithmetic  19.3 us (10%)
  between operations  14.1 us (7%)
  matrix products  7.83 us (4%)
  starting transfers between devices  6.41 us (3%)
    psum x1, blocking collectives, per_device(): lax.psum((partial_gram, weight_sum), ('mem', 'space'))  63.8 us
    all_gather x1, waiting for transfers between devices, per_device(): members_block = lax.all_gather(ensemble, 'mem', axis=0, tiled=True)  42.6 us
    all_to_all x1, waiting for transfers between devices, per_device(): lax.all_to_all(observed.astype(jnp.bfloat16), 'mem', split_axis=2, concat...  25.9 us
    unnamed x9, local copies, waits for them, and re-layouts  10.8 us
    reduce_sum x1, other arithmetic, per_device(): totals = jnp.sum(members_block, axis=0, dtype=jnp.float32)  6.65 us
    convert_element_type x1, local copies, waits for them, and re-layouts, per_device(): by_columns = lax.all_to_all(observed.astype(jnp.bfloat16), 'mem', split_a...  6.59 us
    all_to_all x1, starting transfers between devices, per_device(): lax.all_to_all(observed.astype(jnp.bfloat16), 'mem', split_axis=2, concat...  6.38 us
    convert_element_type x1, other arithmetic, per_device(): by_columns = lax.all_to_all(observed.astype(jnp.bfloat16), 'mem', split_a...  6.11 us
  transfers between devices with their start and end apart: 2, of which 2 were waited for; matrix products, arithmetic and copies ran while one was open for 20% of the time, Pallas kernels for 0%

commit v1 on v0

--- a/solution.py
+++ b/solution.py
@@ -20,7 +20,12 @@
     own_start = lax.axis_index("mem") * local_members
     own_columns = lax.dynamic_slice_in_dim(transform, own_start, local_members, 1)
     keep_mean = 1.0 - jnp.sum(own_columns.astype(jnp.float32), axis=0)
-    members_block = lax.all_gather(ensemble, "mem", axis=0, tiled=True)
+    ring = [ensemble]
+    for hop in range(3):
+        ring.append(lax.ppermute(ring[-1], "mem", [(dev, (dev + 1) % 4) for dev in range(4)]))
+    members_block = jnp.roll(
+        jnp.concatenate(ring[::-1], axis=0), (lax.axis_index("mem") + 1) * ring[0].shape[0], axis=0
+    )
     combined = jnp.einsum(
         "kj,kvc->jvc", own_columns, members_block, preferred_element_type=jnp.float32
     )

time: 203 us -> 285 us (1.40)
  waiting for transfers between devices: 69.2 us -> 144 us
  local copies, waits for them, and re-layouts: 22.2 us -> 41.9 us
  between operations: 14.1 us -> 0.74 us
  blocking collectives: 63.8 us -> 58.9 us
  matrix products: 7.83 us -> 12.3 us
    ppermute x0 -> x3, waiting for transfers between devices: none -> 87.2 us  [per_device(): lax.ppermute(ring[-1], 'mem', [(dev, (dev + 1) % 4) for dev in range(4)])]
    all_gather x1 -> x0, waiting for transfers between devices: 42.6 us -> none  [per_device(): members_block = lax.all_gather(ensemble, 'mem', axis=0, tiled=True)]
    all_to_all x1, waiting for transfers between devices: 25.9 us -> 57.2 us  [per_device(): lax.all_to_all(observed.astype(jnp.bfloat16), 'mem', split_axis=2, concat...]
    unnamed x9 -> x20, local copies, waits for them, and re-layouts: 10.8 us -> 28.9 us
    psum x1, blocking collectives: 63.8 us -> 58.9 us  [per_device(): lax.psum((partial_gram, weight_sum), ('mem', 'space'))]
    dot_general x1, matrix products: 2.79 us -> 6.43 us  [per_device(): jnp.einsum('kj,kvc->jvc', own_columns, members_block, preferred_element_t...]
    ppermute x0 -> x3, starting transfers between devices: none -> 3.11 us  [per_device(): lax.ppermute(ring[-1], 'mem', [(dev, (dev + 1) % 4) for dev in range(4)])]
  transfers between devices with their start and end apart: 2 -> 4, of which waited for: 2 -> 3; matrix products, arithmetic and copies ran while one was open for 20% -> 14% of each run, Pallas kernels for 0% -> 0%
where the time goes in v1:
time: 285 us
  waiting for transfers between devices  144 us (51%)
  blocking collectives  58.9 us (21%)
  local copies, waits for them, and re-layouts  41.9 us (15%)
  other arithmetic  19.2 us (7%)
  matrix products  12.3 us (4%)
  starting transfers between devices  7.36 us (3%)
    ppermute x3, waiting for transfers between devices, per_device(): lax.ppermute(ring[-1], 'mem', [(dev, (dev + 1) % 4) for dev in range(4)])  87.2 us
    psum x1, blocking collectives, per_device(): lax.psum((partial_gram, weight_sum), ('mem', 'space'))  58.9 us
    all_to_all x1, waiting for transfers between devices, per_device(): lax.all_to_all(observed.astype(jnp.bfloat16), 'mem', split_axis=2, concat...  57.2 us
    unnamed x20, local copies, waits for them, and re-layouts  28.9 us
    convert_element_type x1, local copies, waits for them, and re-layouts, per_device(): by_columns = lax.all_to_all(observed.astype(jnp.bfloat16), 'mem', split_a...  6.53 us
    reduce_sum x1, other arithmetic, per_device(): totals = jnp.sum(members_block, axis=0, dtype=jnp.float32)  6.43 us
    dot_general x1, matrix products, per_device(): jnp.einsum('kj,kvc->jvc', own_columns, members_block, preferred_element_t...  6.43 us
    convert_element_type x1, other arithmetic, per_device(): by_columns = lax.all_to_all(observed.astype(jnp.bfloat16), 'mem', split_a...  6.07 us
  transfers between devices with their start and end apart: 4, of which 3 were waited for; matrix products, arithmetic and copies ran while one was open for 14% of the time, Pallas kernels for 0%

profile of v1, /device:TPU:0, one launch (start us, length us, event | category | flops | bytes accessed | tf_op | source)
XLA Modules:
  0.0 284.7 jit_solution(1606655496220426348)
XLA Ops:
  0.6 0.0 copy-start
  0.6 3.1 %collective-permute-start = (bf16[16,70,1024]{2,0,1:T(8,128)(2,1)}, bf16[16,70,1024]{2,0,1:T(8,128)(2,1)S(1)}, u32[]{:S(2)}, u32[]{:S(2)}) collective-permute-start(bf16[16,70,1024]{2,0,1:T(8,128)(2,1)} %param.4), channel_id=1, source_target_pairs={{0,4},{4,8},{8,12},{12,0},{1,5},{5,9},{9,13},{13,1},{2,6},{6,10},{... | collective-permute-start | bytes 6881288 | tf_op jit(solution)/shard_map/ppermute | solution.py:25
  3.8 52.1 %collective-permute-done = bf16[16,70,1024]{2,0,1:T(8,128)(2,1)S(1)} collective-permute-done((bf16[16,70,1024]{2,0,1:T(8,128)(2,1)}, bf16[16,70,1024]{2,0,1:T(8,128)(2,1)S(1)}, u32[]{:S(2)}, u32[]{:S(2)}) %collective-permute-start) | collective-permute-done | bytes 2293792 | tf_op jit(solution)/shard_map/ppermute | solution.py:25
  55.8 0.0 copy-start.2
  55.8 0.0 collective-permute-start.1
  55.8 3.8 %fusion.11 = bf16[16,16,1024]{2,1,0:T(8,128)(2,1)S(1)} fusion(bf16[16,70,1024]{2,0,1:T(8,128)(2,1)} %param.4, bf16[16,70]{1,0:T(8,128)(2,1)} %param.6), kind=kOutput, calls=%fused_computation.10 | convolution fusion | flops 36962304 | bytes 2820288 | tf_op jit(solution)/shard_map/ov,mvc->moc/dot_general | solution.py:38
  59.7 4.7 %copy.25 = bf16[16,16,1024]{1,0,2:T(8,128)(2,1)} copy(bf16[16,16,1024]{2,1,0:T(8,128)(2,1)S(1)} %fusion.11) | data formatting | bytes 1048576 | tf_op jit(solution)/shard_map/convert_element_type | solution.py:40
  64.4 6.5 %reshape.27 = bf16[4,2,32768]{2,1,0:T(2,128)(2,1)} reshape(bf16[1024,16,16]{2,1,0:T(8,128)(2,1)} %bitcast.27) | data formatting | bytes 1048576
  70.8 4.3 %all-to-all-start = ((bf16[4,2,32768]{2,1,0:T(2,128)(2,1)}), bf16[4,2,32768]{2,1,0:T(2,128)(2,1)S(1)}, u32[]{:S(2)}, u32[]{:S(2)}) async-start(bf16[4,2,32768]{2,1,0:T(2,128)(2,1)} %reshape.27), calls=%async_computation | async-start | bytes 1048576 | tf_op jit(solution)/shard_map/all_to_all | solution.py:39
  75.1 0.0 copy-done
  75.1 0.1 constant_dynamic-slice_fusion.1
  75.2 0.1 copy.28
  75.3 0.1 convert_reduce_fusion.2
  75.4 35.1 %collective-permute-done.1 = bf16[16,70,1024]{2,0,1:T(8,128)(2,1)} collective-permute-done((bf16[16,70,1024]{2,0,1:T(8,128)(2,1)S(1)}, bf16[16,70,1024]{2,0,1:T(8,128)(2,1)}, u32[]{:S(2)}, u32[]{:S(2)}) %collective-permute-start.1) | collective-permute-done | bytes 2293792 | tf_op jit(solution)/shard_map/ppermute | solution.py:25
  110.5 0.0 collective-permute-start.2
  110.5 1.3 fusion.21
  111.8 57.2 %all-to-all-done = bf16[4,2,32768]{2,1,0:T(2,128)(2,1)S(1)} async-done(((bf16[4,2,32768]{2,1,0:T(2,128)(2,1)}), bf16[4,2,32768]{2,1,0:T(2,128)(2,1)S(1)}, u32[]{:S(2)}, u32[]{:S(2)}) %all-to-all-start) | async-done | bytes 524320 | tf_op jit(solution)/shard_map/all_to_all | solution.py:39
  169.0 4.1 %reshape.28 = bf16[1024,16,16]{2,1,0:T(8,128)(2,1)} reshape(bf16[4,2,32768]{2,1,0:T(2,128)(2,1)S(1)} %all-to-all-done) | data formatting | bytes 1048576
  173.2 6.1 %bitcast_convert_fusion = f32[16,16,1024]{1,0,2:T(8,128)} fusion(bf16[1024,16,16]{2,1,0:T(8,128)(2,1)} %reshape.28), kind=kLoop, calls=%fused_computation.33 | loop fusion | flops 262144 | bytes 1572864 | tf_op jit(solution)/shard_map/convert_element_type | solution.py:41
  179.3 0.0 copy-done.2
  179.3 6.5 %copy.26 = f32[4,16,16,256]{3,1,0,2:T(8,128)S(1)} copy(f32[4,16,16,256]{2,1,3,0:T(8,128)} %bitcast.26) | data formatting | bytes 2097152 | tf_op jit(solution)/shard_map/convert_element_type | solution.py:41
  185.8 4.2 %convert_reduce_fusion.1 = f32[16,1024]{0,1:T(8,128)S(1)} fusion(bf16[1024,16,16]{2,1,0:T(8,128)(2,1)} %reshape.28), kind=kLoop, calls=%fused_computation.6 | loop fusion | flops 507904 | bytes 589824 | tf_op jit(solution)/shard_map/reduce_sum | solution.py:11
  190.1 0.1 copy.27
  190.1 0.0 copy-start.1
  190.1 0.1 bitcast_subtract_fusion
  190.3 1.0 fusion.14
  191.3 58.9 %all-reduce = (f32[64,64]{1,0:T(8,128)S(1)}, f32[]{:T(128)}) all-reduce(f32[64,64]{1,0:T(8,128)S(1)} %fusion.14, f32[]{:T(128)} %get-tuple-element.5), channel_id=1, replica_groups=mesh['parts'=2,'mem'=4,'space'=4] {'mem','space'}, use_global_device_ids=true, to_apply=%region_4.5 | all-reduce | flops 4097 | bytes 32776 | tf_op jit(solution)/shard_map/psum | solution.py:47
  250.2 0.0 copy-start.3
  250.2 0.8 broadcast_divide_fusion
  251.0 0.0 copy-start.4
  251.0 0.2 fusion.22
  251.2 0.8 fusion.23
  252.1 0.0 collective-permute-done.2
  252.1 3.3 %constant_dynamic-update-slice_fusion.7 = bf16[128,70,1024]{2,0,1:T(8,128)(2,1)} fusion(bf16[16,70,1024]{2,0,1:T(8,128)(2,1)} %collective-permute-done.2), kind=kLoop, calls=%fused_computation.22 | loop fusion | bytes 4587520
  255.4 3.4 %constant_dynamic-update-slice_fusion.6 = bf16[128,70,1024]{2,0,1:T(8,128)(2,1)} fusion(bf16[128,70,1024]{2,0,1:T(8,128)(2,1)} %constant_dynamic-update-slice_fusion.7, bf16[16,70,1024]{2,0,1:T(8,128)(2,1)} %collective-permute-done.1), kind=kLoop, calls=%fused_computation.21 | loop fusion | bytes 4587520
  258.8 0.0 copy-done.3
  258.8 1.6 constant_dynamic-update-slice_fusion.5
  260.4 0.0 copy-done.1
  260.4 1.5 constant_dynamic-update-slice_fusion.4
  262.0 0.0 copy-done.4
  262.0 3.3 %constant_dynamic-update-slice_fusion.3 = bf16[128,70,1024]{2,0,1:T(8,128)(2,1)} fusion(bf16[128,70,1024]{2,0,1:T(8,128)(2,1)} %constant_dynamic-update-slice_fusion.4, bf16[16,70,1024]{2,0,1:T(8,128)(2,1)} %collective-permute-done.2), kind=kLoop, calls=%fused_computation.18 | loop fusion | bytes 4587520
  265.3 3.3 %constant_dynamic-update-slice_fusion.2 = bf16[128,70,1024]{2,0,1:T(8,128)(2,1)} fusion(bf16[128,70,1024]{2,0,1:T(8,128)(2,1)} %constant_dynamic-update-slice_fusion.3, bf16[16,70,1024]{2,0,1:T(8,128)(2,1)} %collective-permute-done.1), kind=kLoop, calls=%fused_computation.17 | loop fusion | bytes 4587520
  268.6 1.6 constant_dynamic-update-slice_fusion.1
  270.3 1.6 constant_dynamic-update-slice_fusion
  271.8 6.4 %convert_reduce_fusion = f32[70,1024]{1,0:T(8,128)S(1)} fusion(bf16[128,70,1024]{2,0,1:T(8,128)(2,1)} %constant_dynamic-update-slice_fusion, s32[]{:T(128)S(6)} %select_n.21), kind=kLoop, calls=%fused_computation | loop fusion | flops 9103360 | bytes 9461764 | tf_op jit(solution)/shard_map/reduce_sum | solution.py:32
  278.3 6.4 %add_convert_fusion = bf16[16,70,1024]{2,0,1:T(8,128)(2,1)} fusion(f32[16]{0:T(128)S(1)} %broadcast_subtract_fusion, f32[70,1024]{1,0:T(8,128)S(1)} %broadcast_multiply_fusion, bf16[128,70,1024]{2,0,1:T(8,128)(2,1)} %constant_dynamic-update-slice_fusion, s32[]{:T(128)S(6)} %select_n.21, bf16[64,16]{1,0:T(8,128)(2,1)S(1)} %constant_dynamic-slice_fusion.1), kind=kOutput, calls=%fused_computation.3 | convolution fusion | flops 150241280 | bytes 11757636 | tf_op jit(solution)/shard_map/kj,kvc->jvc/dot_general | solution.py:29
  (4 shorter events, 0.1 us)
Async XLA Ops:
  0.6 74.5 %copy-start = (bf16[64,64]{1,0:T(8,128)(2,1)S(1)}, bf16[64,64]{1,0:T(8,128)(2,1)}, u32[]{:S(2)}) copy-start(bf16[64,64]{1,0:T(8,128)(2,1)} %param.5) | copy-start | bytes 24580
  0.6 55.2 %collective-permute-start = (bf16[16,70,1024]{2,0,1:T(8,128)(2,1)}, bf16[16,70,1024]{2,0,1:T(8,128)(2,1)S(1)}, u32[]{:S(2)}, u32[]{:S(2)}) collective-permute-start(bf16[16,70,1024]{2,0,1:T(8,128)(2,1)} %param.4), channel_id=1, source_target_pairs={{0,4},{4,8},{8,12},{12,0},{1,5},{5,9},{9,13},{13,1},{2,6},{6,10},{... | collective-permute-start | bytes 6881288 | tf_op jit(solution)/shard_map/ppermute | solution.py:25
  55.8 123.4 %copy-start.2 = (bf16[16,70,1024]{2,0,1:T(8,128)(2,1)}, bf16[16,70,1024]{2,0,1:T(8,128)(2,1)S(1)}, u32[]{:S(2)}) copy-start(bf16[16,70,1024]{2,0,1:T(8,128)(2,1)S(1)} %collective-permute-done) | copy-start | bytes 6881284
  55.8 54.7 %collective-permute-start.1 = (bf16[16,70,1024]{2,0,1:T(8,128)(2,1)S(1)}, bf16[16,70,1024]{2,0,1:T(8,128)(2,1)}, u32[]{:S(2)}, u32[]{:S(2)}) collective-permute-start(bf16[16,70,1024]{2,0,1:T(8,128)(2,1)S(1)} %collective-permute-done), channel_id=1, source_target_pairs={{0,4},{4,8},{8,12},{12,0},{1,5},{5,9},{9,13},{13,1},{2,6},{6,10},{... | collective-permute-start | bytes 6881288 | tf_op jit(solution)/shard_map/ppermute | solution.py:25
  70.8 98.2 %all-to-all-start = ((bf16[4,2,32768]{2,1,0:T(2,128)(2,1)}), bf16[4,2,32768]{2,1,0:T(2,128)(2,1)S(1)}, u32[]{:S(2)}, u32[]{:S(2)}) async-start(bf16[4,2,32768]{2,1,0:T(2,128)(2,1)} %reshape.27), calls=%async_computation | async-start | bytes 1048576 | tf_op jit(solution)/shard_map/all_to_all | solution.py:39
  110.5 141.6 %collective-permute-start.2 = (bf16[16,70,1024]{2,0,1:T(8,128)(2,1)}, bf16[16,70,1024]{2,0,1:T(8,128)(2,1)}, u32[]{:S(2)}, u32[]{:S(2)}) collective-permute-start(bf16[16,70,1024]{2,0,1:T(8,128)(2,1)} %collective-permute-done.1), channel_id=1, source_target_pairs={{0,4},{4,8},{8,12},{12,0},{1,5},{5,9},{9,13},{13,1},{2,6},{6,10},{... | collective-permute-start | bytes 6881288 | tf_op jit(solution)/shard_map/ppermute | solution.py:25
  190.1 70.3 %copy-start.1 = (bf16[16,70,1024]{2,0,1:T(8,128)(2,1)S(1)}, bf16[16,70,1024]{2,0,1:T(8,128)(2,1)}, u32[]{:S(2)}) copy-start(bf16[16,70,1024]{2,0,1:T(8,128)(2,1)} %param.4) | copy-start | bytes 6881284
  250.2 8.6 %copy-start.3 = (bf16[16,70,1024]{2,0,1:T(8,128)(2,1)S(1)}, bf16[16,70,1024]{2,0,1:T(8,128)(2,1)}, u32[]{:S(2)}) copy-start(bf16[16,70,1024]{2,0,1:T(8,128)(2,1)} %copy-done.2) | copy-start | bytes 6881284
  251.0 11.0 %copy-start.4 = (f32[64,64]{1,0:T(8,128)}, f32[64,64]{1,0:T(8,128)S(1)}, u32[]{:S(2)}) copy-start(f32[64,64]{1,0:T(8,128)S(1)} %broadcast_divide_fusion) | copy-start | bytes 49156
